TPU v7x, 32 devices: a whole 2x2x4 slice. The times are simulated.
32 devices in a mesh: replica: 2 (over x), batch: 16 (over z, y, core).
Axes of the slice: x: 2, y: 2, z: 4, core: 2. Of those that a mesh axis runs over, the one named last changes fastest.
Arguments:
- cache_state: bfloat16 [256, 12, 64, 128], P(('replica', 'batch')), parts along dimension 0, may hold values from -6 to 6
- prefill_state: bfloat16 [64, 12, 64, 128], P(('replica', 'batch')), parts along dimension 0, may hold values from -6 to 6
- x_in: bfloat16 [256, 768], P(('replica', 'batch')), parts along dimension 0, may hold values from -6 to 6
- z_in: bfloat16 [256, 768], P(('replica', 'batch')), parts along dimension 0, may hold values from -6 to 6
- b_in: bfloat16 [256, 128], P(('replica', 'batch')), parts along dimension 0, may hold values from -6 to 6
- c_in: bfloat16 [256, 128], P(('replica', 'batch')), parts along dimension 0, may hold values from -0.59765625 to 0.59765625
- dt_in: bfloat16 [256, 12], P(('replica', 'batch')), parts along dimension 0, may hold values from -4 to 4
- dt_bias: float32 [12], replicated, may hold values from -3 to 0.5
- a_log: float32 [12], replicated, may hold values from 0 to 2.5
- d_skip: float32 [12], replicated, may hold values from 0.5 to 1.5
- norm_gain: float32 [768], replicated, may hold values from 0.25 to 1.75
- out_weight: bfloat16 [768, 4096], replicated, may hold values from -0.21875 to 0.21875
- active: int32 [256], P(('replica', 'batch')), parts along dimension 0, may hold values from 0 to 1, as said below
- prefill_count: int32 [32], P(('replica', 'batch')), parts along dimension 0, may hold values from 0 to 2, as said below
- dest_owner: int32 [64], P(('replica', 'batch')), parts along dimension 0, may hold values from 0 to 15, as said below
- dest_slot: int32 [64], P(('replica', 'batch')), parts along dimension 0, may hold values from 0 to 7, as said below
Outputs:
- mixed: bfloat16 [256, 4096], P(('replica', 'batch')), parts along dimension 0
- new_state: bfloat16 [256, 12, 64, 128], P(('replica', 'batch')), parts along dimension 0
There are 2 independent parts, one for each index of `replica`. A program takes and returns all parts, laid end to end along the dimension named above; an argument that names none is the same for every part. Nothing has to cross between parts.
Inputs may be any that keep to these rules, and one draw needn't show every extreme that they name: `active`: at least 2 slots of every device are 0. `prefill_count`: the live rows of a device are its first ones. `dest_owner`: for each row index j below 2, the rows j of the devices go to distinct owners; the two rows of one device go to different owners. So an owner receives at most 2 live rows, at most one from any device, and some owner exactly 2. `dest_slot`: A live row's slot is 0 in the owner's active entries, and no two live rows share an owner and slot.
All inputs are finite; a program needn't handle non-finite values.
Results may differ from a plain program's by a relative error of at most 0.0049.
Values may be sent and summed in bfloat16 or wider, within the bound.
A program may use at most 128 MiB of HBM per device.

v0:
```python
import jax
import jax.numpy as jnp
from jax import lax
from jax.sharding import PartitionSpec as P


def advance(
    state, x_in, z_in, b_in, c_in, dt_in, dt_bias, a_log, d_skip, norm_gain, out_weight, live
):
    rows, heads, hdim, nstate = state.shape
    step = jax.nn.softplus(dt_in.astype(jnp.float32) + dt_bias[None, :])
    decay = jnp.exp(-step * jnp.exp(a_log)[None, :])
    inputs = x_in.astype(jnp.float32).reshape(rows, heads, hdim)
    b_vals = b_in.astype(jnp.float32)
    c_vals = c_in.astype(jnp.float32)
    fresh = (
        state * decay[:, :, None, None]
        + (step[:, :, None] * inputs)[:, :, :, None] * b_vals[:, None, None, :]
    )
    ys = (
        jnp.einsum("rhpn,rn->rhp", fresh, c_vals, precision=lax.Precision.HIGHEST)
        + d_skip[None, :, None] * inputs
    )
    gated = ys.reshape(rows, heads * hdim) * jax.nn.silu(z_in.astype(jnp.float32))
    scale = lax.rsqrt(jnp.mean(gated * gated, axis=1, keepdims=True) + 1e-05)
    normed = jnp.where(live[:, None], gated * scale * norm_gain[None, :], 0.0).astype(jnp.bfloat16)
    mixed = jnp.dot(normed, out_weight, preferred_element_type=jnp.float32).astype(jnp.bfloat16)
    new_state = jnp.where(live[:, None, None, None], fresh, 0.0).astype(jnp.bfloat16)
    return (mixed, new_state)


def body(
    cache_state,
    prefill_state,
    x_in,
    z_in,
    b_in,
    c_in,
    dt_in,
    dt_bias,
    a_log,
    d_skip,
    norm_gain,
    out_weight,
    active,
    prefill_count,
    dest_owner,
    dest_slot,
):
    myself = lax.axis_index("batch")
    slots, heads, hdim, nstate = cache_state.shape
    fresh_rows = prefill_state.shape[0]
    valid = jnp.arange(fresh_rows, dtype=jnp.int32) < prefill_count[0]
    owner_local = jnp.where(valid, dest_owner, -1)
    owner_all, slot_all = (
        lax.all_gather(owner_local, "batch", axis=0, tiled=True),
        lax.all_gather(dest_slot, "batch", axis=0, tiled=True),
    )
    slot_ids = jnp.arange(slots, dtype=jnp.int32)
    onehot = ((owner_all[None, :] == myself) & (slot_all[None, :] == slot_ids[:, None])).astype(
        jnp.bfloat16
    )
    moved = jnp.einsum(
        "sr,rhpn->shpn",
        onehot,
        lax.all_gather(prefill_state, "batch", axis=0, tiled=True),
        preferred_element_type=jnp.float32,
    )
    arrived = jnp.sum(onehot.astype(jnp.float32), axis=1)
    landed = arrived > 0.5
    live = (active > 0) | landed
    state = jnp.where(landed[:, None, None, None], moved, cache_state.astype(jnp.float32))
    return advance(
        state, x_in, z_in, b_in, c_in, dt_in, dt_bias, a_log, d_skip, norm_gain, out_weight, live
    )


def solution(mesh):
    in_specs = (
        P(("replica", "batch"), None, None, None),
        P(("replica", "batch"), None, None, None),
        P(("replica", "batch"), None),
        P(("replica", "batch"), None),
        P(("replica", "batch"), None),
        P(("replica", "batch"), None),
        P(("replica", "batch"), None),
        P(),
        P(),
        P(),
        P(),
        P(),
        P(("replica", "batch")),
        P(("replica", "batch")),
        P(("replica", "batch")),
        P(("replica", "batch")),
    )
    out_specs = (P(("replica", "batch"), None), P(("replica", "batch"), None, None, None))
    return jax.shard_map(body, mesh=mesh, in_specs=in_specs, out_specs=out_specs, check_vma=False)
```

profile of v0, /device:TPU:0, one launch (start us, length us, event | category | flops | bytes accessed | tf_op | source)
XLA Modules:
  0.0 99.9 jit_solution(15233405479906847518)
XLA Ops:
  7.2 0.0 copy-start
  7.2 0.0 all-gather.2.cloned.1.call-start
  7.2 0.7 all-gather.2.cloned.1.call-update
  8.6 0.7 exp.15
  9.2 0.7 convert_element_type.33
  9.9 0.7 multiply_exponential_fusion
  10.6 0.1 copy.31
  10.7 0.8 reshape.45
  11.5 0.1 broadcast_multiply_fusion
  11.6 0.2 copy.32
  11.8 1.2 %dynamic-slice = u32[1]{0:T(128)} dynamic-slice(u32[32]{0:T(128)} %constant.35, u32[]{:T(128)S(6)} %add.37), dynamic_slice_sizes={1} | dynamic-slice | bytes 12
  13.7 0.9 dynamic-update-slice.1
  14.6 0.7 fusion.21
  15.3 13.8 %all-reduce.2 = (s32[32]{0:T(128)S(1)}, s32[32]{0:T(128)S(1)}) all-reduce(s32[32]{0:T(128)S(1)} %dynamic-update-slice.1, s32[32]{0:T(128)S(1)} %fusion.21), channel_id=1, replica_groups=mesh['replica'=2,'batch'=16] {'batch'}, use_global_device_ids=true, to_apply=%add.1 | all-reduce | flops 64 | bytes 512
  29.1 0.1 convert_reduce_fusion
  29.3 0.7 compare_or_fusion
  29.9 44.6 %all-gather.2.cloned.1.call-done = bf16[32,12,64,128]{3,2,1,0:T(8,128)(2,1)} async-done(((bf16[2,12,64,128]{3,2,1,0:T(8,128)(2,1)}), bf16[32,12,64,128]{3,2,1,0:T(8,128)(2,1)}) %all-gather.2.cloned.1.call-update) | async-done | bytes 6291472 | tf_op jit(solution)/shard_map/all_gather | solution.py:66
  74.5 8.4 %select_convert_fusion = (bf16[8,12,64,128]{3,0,2,1:T(8,128)(2,1)S(1)}, f32[8,12,64,128]{3,0,2,1:T(8,128)S(1)}) fusion(pred[8]{0:T(512)(128)(4,1)S(1)} %get-tuple-element.12, f32[8,128]{1,0:T(8,128)S(1)} %convert_element_type.33, f32[8,12,64]{0,2,1:T(8,128)S(1)} %copy.32, f32[8,12]{0,1:T(8,128)S(1)} %copy.31, bf16[8,12,64,128]{3,2,1,0:T(8,128)(2,1)} %param.16, ...), kind=kOutput, calls=%fused_computation.5 | convolution fusion | flops 55050752 | bytes 12612144 | tf_op jit(solution)/shard_map/sr,rhpn->shpn/dot_general | solution.py:63
  83.0 0.0 copy-start.3
  83.0 0.0 copy-start.1
  83.0 0.0 copy-start.2
  83.0 1.6 %copy.33 = bf16[8,12,64,128]{3,2,1,0:T(8,128)(2,1)} copy(bf16[8,12,64,128]{3,0,2,1:T(8,128)(2,1)S(1)} %get-tuple-element.14) | data formatting | bytes 3145728
  84.6 0.0 copy-done
  84.6 3.8 %fusion.2 = f32[8,1,12,64]{3,1,2,0:T(1,128)S(1)} fusion(f32[8,12,64,128]{3,0,2,1:T(8,128)S(1)} %get-tuple-element.15, bf16[8,128,1,1]{1,0,2,3:T(8,128)(2,1)S(1)} %bitcast.14), kind=kOutput, calls=%fused_computation.3 | convolution fusion | flops 9437184 | bytes 3172352 | tf_op jit(solution)/shard_map/rhpn,rn->rhp/dot_general | solution.py:21
  88.3 0.0 copy-done.3
  88.3 0.1 bitcast_add_fusion
  88.4 0.1 reshape.43
  88.5 0.0 copy-done.1
  88.5 0.1 multiply_reduce_fusion
  88.7 0.0 copy-done.2
  88.7 4.4 %convolution_convert_fusion = bf16[8,4096]{1,0:T(8,128)(2,1)} fusion(bf16[768,4096]{1,0:T(8,128)(2,1)} %param.27, f32[768]{0:T(1024)S(1)} %copy-done.2, f32[8]{0:T(128)S(1)} %add_rsqrt_fusion, pred[8]{0:T(512)(128)(4,1)S(1)} %get-tuple-element.12, f32[8,768]{1,0:T(8,128)S(1)} %reshape.43, bf16[8,768]{1,0:T(8,128)(2,1)S(1)} %copy-done.1), kind=kOutput, calls=%fused_computation.2 | convolution fusion | flops 50425856 | bytes 6396968 | tf_op jit(solution)/shard_map/dot_general | solution.py:27
  (4 shorter events, 0.0 us)
Async XLA Ops:
  7.2 77.4 %copy-start = (bf16[8,128]{1,0:T(8,128)(2,1)S(1)}, bf16[8,128]{1,0:T(8,128)(2,1)}, u32[]{:S(2)}) copy-start(bf16[8,128]{1,0:T(8,128)(2,1)} %param.21) | copy-start | bytes 6148
  7.2 67.3 %all-gather.2.cloned.1.call-start = ((), (), s32[]{:S(2)}) async-start(), calls=%async_computation | async-start | bytes 6684672 | tf_op jit(solution)/shard_map/all_gather | solution.py:66
  83.0 5.4 %copy-start.3 = (f32[12]{0:T(128)S(1)}, f32[12]{0:T(128)}, u32[]{:S(2)}) copy-start(f32[12]{0:T(128)} %param.25) | copy-start | bytes 148
  83.0 5.5 %copy-start.1 = (bf16[8,768]{1,0:T(8,128)(2,1)S(1)}, bf16[8,768]{1,0:T(8,128)(2,1)}, u32[]{:S(2)}) copy-start(bf16[8,768]{1,0:T(8,128)(2,1)} %param.19) | copy-start | bytes 36868
  83.0 5.7 %copy-start.2 = (f32[768]{0:T(1024)S(1)}, f32[768]{0:T(1024)}, u32[]{:S(2)}) copy-start(f32[768]{0:T(1024)} %param.26) | copy-start | bytes 9220
Sparse Core Ops, SparseCore 0:
  10.3 64.2 all-gather.1
where the time goes:
time: 100 us; the launch traced here: 99.9 us
  waiting for transfers between devices  45.3 us (45%)
  matrix products  16.6 us (17%)
  between operations  15.4 us (15%)
  blocking collectives  13.8 us (14%)
  local copies, waits for them, and re-layouts  5.49 us (5%)
  other arithmetic  3.25 us (3%)
    all_gather x1, waiting for transfers between devices, body(): lax.all_gather(prefill_state, 'batch', axis=0, tiled=True)  44.6 us
    unnamed x1, blocking collectives  13.8 us
    dot_general x1, matrix products, body(): jnp.einsum('sr,rhpn->shpn', onehot, lax.all_gather(prefill_state, 'batch'...  8.45 us
    dot_general x1, matrix products, advance(): jnp.dot(normed, out_weight, preferred_element_type=jnp.float32)  4.39 us
    dot_general x1, matrix products, advance(): jnp.einsum('rhpn,rn->rhp', fresh, c_vals, precision=lax.Precision.HIGHEST)  3.76 us
    unnamed x13, local copies, waits for them, and re-layouts  3.69 us
  transfers between devices with their start and end apart: 1, of which 1 were waited for; matrix products, arithmetic and copies ran while one was open for 7% of the time, Pallas kernels for 0%

commit v1 on v0

--- a/solution.py
+++ b/solution.py
@@ -63,7 +63,10 @@
     moved = jnp.einsum(
         "sr,rhpn->shpn",
         onehot,
-        lax.all_gather(prefill_state, "batch", axis=0, tiled=True),
+        jnp.concatenate(
+            lax.all_to_all(jnp.stack([prefill_state] * lax.axis_size("batch")), "batch", 0, 0),
+            axis=0,
+        ),
         preferred_element_type=jnp.float32,
     )
     arrived = jnp.sum(onehot.astype(jnp.float32), axis=1)

time: 100 us -> 174 us (1.74)
  blocking collectives: 13.8 us -> 136 us
  waiting for transfers between devices: 45.3 us -> 0.01 us
  between operations: 15.4 us -> 2.22 us
  local copies, waits for them, and re-layouts: 5.49 us -> 15.9 us
  starting transfers between devices: 0.04 us -> 7.6 us
  matrix products: 16.6 us -> 10.6 us
  other arithmetic: 3.25 us -> 1.12 us
    unnamed x1, blocking collectives: 13.8 us -> 136 us
    all_gather x1 -> x0, waiting for transfers between devices: 44.6 us -> none  [body(): lax.all_gather(prefill_state, 'batch', axis=0, tiled=True)]
    all_to_all x0 -> x1, starting transfers between devices: none -> 7.6 us  [body(): lax.all_to_all(jnp.stack([prefill_state] * lax.axis_size('batch')), 'batc...]
    dot_general x1, matrix products: 8.45 us -> 2.48 us  [body(): jnp.einsum('sr,rhpn->shpn', onehot, jnp.concatenate(lax.all_to_all(jnp.st...]
    another operation x0 -> x1, local copies, waits for them, and re-layouts: none -> 5.82 us  [body(): jnp.stack([prefill_state] * lax.axis_size('batch'))]
    all_to_all x0 -> x1, local copies, waits for them, and re-layouts: none -> 5.77 us  [body(): lax.all_to_all(jnp.stack([prefill_state] * lax.axis_size('batch')), 'batc...]
    unnamed x13 -> x48, local copies, waits for them, and re-layouts: 3.69 us -> 3.93 us
  transfers between devices with their start and end apart: 1 -> 1, of which waited for: 1 -> 0; matrix products, arithmetic and copies ran while one was open for 7% -> 1% of each run, Pallas kernels for 0% -> 0%
where the time goes in v1:
time: 174 us
  blocking collectives  136 us (78%)
  local copies, waits for them, and re-layouts  15.9 us (9%)
  matrix products  10.6 us (6%)
  starting transfers between devices  7.6 us (4%)
  between operations  2.22 us (1%)
    unnamed x1, blocking collectives  136 us
    all_to_all x1, starting transfers between devices, body(): lax.all_to_all(jnp.stack([prefill_state] * lax.axis_size('batch')), 'batc...  7.6 us
    another operation x1, local copies, waits for them, and re-layouts, body(): jnp.stack([prefill_state] * lax.axis_size('batch'))  5.82 us
    all_to_all x1, local copies, waits for them, and re-layouts, body(): lax.all_to_all(jnp.stack([prefill_state] * lax.axis_size('batch')), 'batc...  5.77 us
    dot_general x1, matrix products, advance(): jnp.dot(normed, out_weight, preferred_element_type=jnp.float32)  4.38 us
    unnamed x48, local copies, waits for them, and re-layouts  3.93 us
    dot_general x1, matrix products, advance(): jnp.einsum('rhpn,rn->rhp', fresh, c_vals, precision=lax.Precision.HIGHEST)  3.76 us
  transfers between devices with their start and end apart: 1, of which 0 were waited for; matrix products, arithmetic and copies ran while one was open for 1% of the time, Pallas kernels for 0%

profile of v1, /device:TPU:0, one launch (start us, length us, event | category | flops | bytes accessed | tf_op | source)
XLA Modules:
  0.0 173.8 jit_solution(13123821720947897466)
XLA Ops:
  0.6 0.0 copy-start
  0.6 1.4 copy.29
  2.1 5.8 %stack.2 = bf16[16,2,12,64,128]{4,1,3,2,0:T(2,128)(2,1)} broadcast(bf16[2,12,64,128]{3,0,2,1:T(2,128)(2,1)S(1)} %copy.29), dimensions={1,2,3,4} | broadcast | bytes 6684672 | tf_op jit(solution)/shard_map/stack | solution.py:67
  7.9 0.0 copy-start.10
  7.9 0.0 copy-start.20
  7.9 0.0 copy-start.19
  7.9 0.0 copy-start.16
  7.9 0.0 copy-start.17
  8.0 7.6 %all-to-all-start = ((bf16[16,2,12,64,128]{4,1,3,2,0:T(2,128)(2,1)}), bf16[16,2,12,64,128]{4,1,3,2,0:T(2,128)(2,1)}, u32[]{:S(2)}, u32[]{:S(2)}) async-start(bf16[16,2,12,64,128]{4,1,3,2,0:T(2,128)(2,1)} %stack.2), calls=%async_computation | async-start | bytes 12582912 | tf_op jit(solution)/shard_map/all_to_all | solution.py:67
  16.2 0.1 reshape.51
  16.4 0.1 broadcast_multiply_fusion
  16.5 0.2 copy.33
  16.7 0.1 copy.32
  16.7 0.6 dynamic-slice
  18.0 0.2 dynamic-update-slice.1
  18.3 0.1 fusion.17
  18.3 136.3 %all-reduce.2 = (s32[32]{0:T(128)S(1)}, s32[32]{0:T(128)S(1)}) all-reduce(s32[32]{0:T(128)S(1)} %dynamic-update-slice.1, s32[32]{0:T(128)S(1)} %fusion.17), channel_id=1, replica_groups=mesh['replica'=2,'batch'=16] {'batch'}, use_global_device_ids=true, to_apply=%add.1 | all-reduce | flops 64 | bytes 512
  154.7 0.1 convert_reduce_fusion
  154.8 0.6 compare_or_fusion
  155.4 5.8 %copy.30 = bf16[16,2,12,64,128]{4,1,0,3,2:T(2,128)(2,1)S(1)} copy(bf16[16,2,12,64,128]{4,1,3,2,0:T(2,128)(2,1)} %all-to-all-done) | data formatting | bytes 12582912 | tf_op jit(solution)/shard_map/all_to_all | solution.py:67
  161.2 2.5 %select_convert_fusion = (bf16[8,12,64,128]{3,0,2,1:T(8,128)(2,1)S(1)}, f32[8,12,64,128]{3,0,2,1:T(8,128)S(1)}) fusion(pred[8]{0:T(512)(128)(4,1)S(1)} %copy-done.6, f32[8,128]{1,0:T(8,128)S(1)} %convert_element_type.33, f32[8,12,64]{0,2,1:T(8,128)S(1)} %copy.33, f32[8,12]{0,1:T(8,128)S(1)} %copy.32, bf16[8,12,64,128]{3,2,1,0:T(8,128)(2,1)S(1)} %copy-done.1, ...), kind=kOutput, calls=%fused_computation.3 | convolution fusion | flops 55050752 | bytes 12612144 | tf_op jit(solution)/shard_map/sr,rhpn->shpn/dot_general | solution.py:63
  163.7 0.0 copy-start.3
  163.7 0.0 copy-start.12
  163.7 0.0 copy-start.4
  163.8 0.0 copy-start.8
  163.8 3.8 %fusion = f32[8,1,12,64]{3,1,2,0:T(1,128)S(1)} fusion(f32[8,12,64,128]{3,0,2,1:T(8,128)S(1)} %get-tuple-element.15, bf16[8,128,1,1]{1,0,2,3:T(8,128)(2,1)S(1)} %bitcast.16), kind=kOutput, calls=%fused_computation.1 | convolution fusion | flops 9437184 | bytes 3172352 | tf_op jit(solution)/shard_map/rhpn,rn->rhp/dot_general | solution.py:21
  167.5 0.0 copy-done.12
  167.6 0.1 bitcast_add_fusion
  167.6 0.1 reshape.49
  167.7 0.1 multiply_reduce_fusion
  167.9 1.6 copy.34
  169.4 4.4 %convolution_convert_fusion = bf16[8,4096]{1,0:T(8,128)(2,1)} fusion(bf16[768,4096]{1,0:T(8,128)(2,1)} %param.27, f32[768]{0:T(1024)S(1)} %copy-done.8, f32[8]{0:T(128)S(1)} %add_rsqrt_fusion, pred[8]{0:T(512)(128)(4,1)S(1)} %copy-done.7, f32[8,768]{1,0:T(8,128)S(1)} %reshape.49, bf16[8,768]{1,0:T(8,128)(2,1)S(1)} %copy-done.4), kind=kOutput, calls=%fused_computation | convolution fusion | flops 50425856 | bytes 6396968 | tf_op jit(solution)/shard_map/dot_general | solution.py:27
  (39 shorter events, 0.1 us)
Async XLA Ops:
  0.6 163.1 %copy-start = (bf16[8,128]{1,0:T(8,128)(2,1)S(1)}, bf16[8,128]{1,0:T(8,128)(2,1)}, u32[]{:S(2)}) copy-start(bf16[8,128]{1,0:T(8,128)(2,1)} %param.21) | copy-start | bytes 6148
  7.9 8.3 %copy-start.5 = (bf16[8,768]{1,0:T(8,128)(2,1)S(1)}, bf16[8,768]{1,0:T(8,128)(2,1)}, u32[]{:S(2)}) copy-start(bf16[8,768]{1,0:T(8,128)(2,1)} %param.18) | copy-start | bytes 36868
  7.9 8.4 %copy-start.18 = (f32[12]{0:T(128)S(1)}, f32[12]{0:T(128)}, u32[]{:S(2)}) copy-start(f32[12]{0:T(128)} %param.24) | copy-start | bytes 148
  7.9 8.5 %copy-start.11 = (bf16[8,12]{1,0:T(8,128)(2,1)S(1)}, bf16[8,12]{1,0:T(8,128)(2,1)}, u32[]{:S(2)}) copy-start(bf16[8,12]{1,0:T(8,128)(2,1)} %param.22) | copy-start | bytes 580
  7.9 8.5 %copy-start.15 = (f32[12]{0:T(128)S(1)}, f32[12]{0:T(128)}, u32[]{:S(2)}) copy-start(f32[12]{0:T(128)} %param.23) | copy-start | bytes 148
  7.9 8.8 %copy-start.10 = (bf16[8,128]{1,0:T(8,128)(2,1)S(1)}, bf16[8,128]{1,0:T(8,128)(2,1)}, u32[]{:S(2)}) copy-start(bf16[8,128]{1,0:T(8,128)(2,1)} %param.20) | copy-start | bytes 6148
  7.9 8.8 %copy-start.20 = (u32[32]{0:T(128)S(1)}, u32[32]{0:T(128)}, u32[]{:S(2)}) copy-start(u32[32]{0:T(128)} %constant.35) | copy-start | bytes 388
  7.9 10.1 %copy-start.19 = (s32[2]{0:T(128)S(1)}, s32[2]{0:T(128)}, u32[]{:S(2)}) copy-start(s32[2]{0:T(128)} %param.31) | copy-start | bytes 28
  7.9 10.3 %copy-start.16 = (s32[2]{0:T(128)S(1)}, s32[2]{0:T(128)}, u32[]{:S(2)}) copy-start(s32[2]{0:T(128)} %param.30) | copy-start | bytes 28
  7.9 146.9 %copy-start.17 = (s32[8]{0:T(128)S(1)}, s32[8]{0:T(128)}, u32[]{:S(2)}) copy-start(s32[8]{0:T(128)} %param.28) | copy-start | bytes 100
  8.0 147.4 %all-to-all-start = ((bf16[16,2,12,64,128]{4,1,3,2,0:T(2,128)(2,1)}), bf16[16,2,12,64,128]{4,1,3,2,0:T(2,128)(2,1)}, u32[]{:S(2)}, u32[]{:S(2)}) async-start(bf16[16,2,12,64,128]{4,1,3,2,0:T(2,128)(2,1)} %stack.2), calls=%async_computation | async-start | bytes 12582912 | tf_op jit(solution)/shard_map/all_to_all | solution.py:67
  16.3 144.9 %copy-start.2 = (f32[8,12,64]{2,1,0:T(8,128)}, f32[8,12,64]{2,1,0:T(8,128)S(1)}, u32[]{:S(2)}) copy-start(f32[8,12,64]{2,1,0:T(8,128)S(1)} %reshape.51) | copy-start | bytes 73732
  154.7 6.5 %copy-start.13 = (s32[32]{0:T(128)}, s32[32]{0:T(128)S(1)}, u32[]{:S(2)}) copy-start(s32[32]{0:T(128)S(1)} %get-tuple-element.8) | copy-start | bytes 388
  154.7 6.5 %copy-start.14 = (pred[32]{0:T(512)(128)(4,1)}, pred[32]{0:T(512)(128)(4,1)S(1)}, u32[]{:S(2)}) copy-start(pred[32]{0:T(512)(128)(4,1)S(1)} %broadcast_compare_fusion.1) | copy-start | bytes 100
  155.4 5.8 %copy-start.1 = (bf16[8,12,64,128]{3,2,1,0:T(8,128)(2,1)S(1)}, bf16[8,12,64,128]{3,2,1,0:T(8,128)(2,1)}, u32[]{:S(2)}) copy-start(bf16[8,12,64,128]{3,2,1,0:T(8,128)(2,1)} %param.16) | copy-start | bytes 4718596
  155.4 5.8 %copy-start.6 = (pred[8]{0:T(512)(128)(4,1)S(1)}, pred[8]{0:T(512)(128)(4,1)}, u32[]{:S(2)}) copy-start(pred[8]{0:T(512)(128)(4,1)} %get-tuple-element.12) | copy-start | bytes 28
  155.4 5.8 %copy-start.9 = (pred[8]{0:T(512)(128)(4,1)S(1)}, pred[8]{0:T(512)(128)(4,1)}, u32[]{:S(2)}) copy-start(pred[8]{0:T(512)(128)(4,1)} %get-tuple-element.13) | copy-start | bytes 28
  163.7 3.8 %copy-start.3 = (f32[8,12,64]{2,1,0:T(8,128)S(1)}, f32[8,12,64]{2,1,0:T(8,128)}, u32[]{:S(2)}) copy-start(f32[8,12,64]{2,1,0:T(8,128)} %copy-done.2) | copy-start | bytes 73732
  163.7 3.8 %copy-start.12 = (f32[12]{0:T(128)S(1)}, f32[12]{0:T(128)}, u32[]{:S(2)}) copy-start(f32[12]{0:T(128)} %param.25) | copy-start | bytes 148
  163.7 4.0 %copy-start.4 = (bf16[8,768]{1,0:T(8,128)(2,1)S(1)}, bf16[8,768]{1,0:T(8,128)(2,1)}, u32[]{:S(2)}) copy-start(bf16[8,768]{1,0:T(8,128)(2,1)} %param.19) | copy-start | bytes 36868
  163.8 5.7 %copy-start.7 = (pred[8]{0:T(512)(128)(4,1)S(1)}, pred[8]{0:T(512)(128)(4,1)}, u32[]{:S(2)}) copy-start(pred[8]{0:T(512)(128)(4,1)} %get-tuple-element.12) | copy-start | bytes 28
  163.8 5.7 %copy-start.8 = (f32[768]{0:T(1024)S(1)}, f32[768]{0:T(1024)}, u32[]{:S(2)}) copy-start(f32[768]{0:T(1024)} %param.26) | copy-start | bytes 9220
